TPU v7x, 32 devices: a whole 2x2x4 slice. The times are simulated.
32 devices in a mesh: rep: 4 (over x, y), dp: 8 (over z, core).
Axes of the slice: x: 2, y: 2, z: 4, core: 2. Of those that a mesh axis runs over, the one named last changes fastest.
Arguments:
- g_w_gate: bfloat16 [32, 2, 1280, 4096], P(('rep', 'dp')), parts along dimension 0
- g_w_up: bfloat16 [32, 2, 1280, 4096], P(('rep', 'dp')), parts along dimension 0
- g_w_down: bfloat16 [32, 2, 4096, 1280], P(('rep', 'dp')), parts along dimension 0
- w_gate: bfloat16 [2, 1280, 4096], replicated
- w_up: bfloat16 [2, 1280, 4096], replicated
- w_down: bfloat16 [2, 4096, 1280], replicated
- m_w_gate: float32 [2, 1280, 4096], P(None, 'dp')
- m_w_up: float32 [2, 1280, 4096], P(None, 'dp')
- m_w_down: float32 [2, 4096, 1280], P(None, 'dp')
- v_w_gate: float32 [2, 1280, 4096], P(None, 'dp')
- v_w_up: float32 [2, 1280, 4096], P(None, 'dp')
- v_w_down: float32 [2, 4096, 1280], P(None, 'dp')
Outputs:
- output 1: bfloat16 [8, 1280, 4096], P('rep'), parts along dimension 0
- output 2: bfloat16 [8, 1280, 4096], P('rep'), parts along dimension 0
- output 3: bfloat16 [8, 4096, 1280], P('rep'), parts along dimension 0
- output 4: float32 [8, 1280, 4096], P('rep', 'dp'), parts along dimension 0
- output 5: float32 [8, 1280, 4096], P('rep', 'dp'), parts along dimension 0
- output 6: float32 [8, 4096, 1280], P('rep', 'dp'), parts along dimension 0
- output 7: float32 [8, 1280, 4096], P('rep', 'dp'), parts along dimension 0
- output 8: float32 [8, 1280, 4096], P('rep', 'dp'), parts along dimension 0
- output 9: float32 [8, 4096, 1280], P('rep', 'dp'), parts along dimension 0
There are 4 independent parts. A program takes and returns all parts, laid end to end along the dimension named above; an argument that names none is the same for every part.
All inputs are finite; a program needn't handle non-finite values.
Results may differ from a plain program's by a relative error of at most 0.022.
Values are sent between devices in bfloat16 or wider.
A program may use at most 2 GiB of HBM per device.

v0:
```python
import jax
import jax.numpy as jnp
from jax import lax
from jax.sharding import PartitionSpec as P


def adamw(w, m, v, g):
    m = 0.9 * m + 0.1 * g
    v = 0.95 * v + 0.05 * g * g
    step = m * lax.rsqrt(v + 1e-8) + 0.1 * w
    return (w - 0.02 * step).astype(jnp.bfloat16), m, v


def solution(mesh):
    def step(*arrays):
        terms, weights, m, v = (arrays[i : i + 3] for i in (0, 3, 6, 9))
        gradients = [lax.psum_scatter(t[0], "dp", scatter_dimension=1, tiled=True).astype(jnp.float32) for t in terms]
        me = lax.axis_index("dp")
        own = [lax.dynamic_slice_in_dim(w, me * one.shape[1], one.shape[1], 1).astype(jnp.float32) for w, one in zip(weights, m, strict=True)]
        new = [adamw(w, m, v, g) for w, m, v, g in zip(own, m, v, gradients, strict=True)]
        whole = [lax.all_gather(one[0], "dp", axis=1, tiled=True) for one in new]
        return (*whole, *(one[1] for one in new), *(one[2] for one in new))

    all_of, cut = P(None, None, None), P(None, "dp", None)
    return jax.shard_map(
        step,
        mesh=mesh,
        in_specs=(P(("rep", "dp"), None, None, None),) * 3 + (all_of,) * 3 + (cut,) * 6,
        out_specs=(P("rep", None, None),) * 3 + (P("rep", "dp", None),) * 6,
        check_vma=False,
    )
```

profile of v0, /device:TPU:0, one launch (start us, length us, event | category | flops | bytes accessed | tf_op | source)
XLA Modules:
  0.0 1246.2 jit_solution(17550120983190017655)
XLA Ops:
  7.2 0.0 reduce-scatter.8.cloned.1.call-start
  7.2 0.7 reduce-scatter.8.cloned.1.call-update
  7.9 0.0 reduce-scatter.6.cloned.1.call-start
  8.0 0.7 reduce-scatter.6.cloned.1.call-update
  8.7 0.0 reduce-scatter.4.cloned.1.call-start
  8.7 0.7 reduce-scatter.4.cloned.1.call-update
  9.4 0.0 all-gather.8.cloned.1.call-start
  9.4 211.1 %reduce-scatter.8.cloned.1.call-done = bf16[2,512,1280]{2,1,0:T(8,128)(2,1)} async-done(((bf16[2,4096,1280]{2,1,0:T(8,128)(2,1)}), bf16[2,512,1280]{2,1,0:T(8,128)(2,1)}) %reduce-scatter.8.cloned.1.call-update) | async-done | bytes 2621456 | tf_op jit(solution)/shard_map/reduce_scatter | solution.py:17
  220.6 10.8 fusion.10
  231.3 0.0 all-gather.8.cloned.1.call-update
  231.4 0.0 all-gather.6.cloned.1.call-start
  231.4 197.7 %reduce-scatter.6.cloned.1.call-done = bf16[2,160,4096]{2,1,0:T(8,128)(2,1)} async-done(((bf16[2,1280,4096]{2,1,0:T(8,128)(2,1)}), bf16[2,160,4096]{2,1,0:T(8,128)(2,1)}) %reduce-scatter.6.cloned.1.call-update) | async-done | bytes 2621456 | tf_op jit(solution)/shard_map/reduce_scatter | solution.py:17
  429.1 10.6 fusion.6
  439.7 0.0 all-gather.6.cloned.1.call-update
  439.8 0.0 all-gather.4.cloned.1.call-start
  439.8 197.9 %reduce-scatter.4.cloned.1.call-done = bf16[2,160,4096]{2,1,0:T(8,128)(2,1)} async-done(((bf16[2,1280,4096]{2,1,0:T(8,128)(2,1)}), bf16[2,160,4096]{2,1,0:T(8,128)(2,1)}) %reduce-scatter.4.cloned.1.call-update) | async-done | bytes 2621456 | tf_op jit(solution)/shard_map/reduce_scatter | solution.py:17
  637.7 10.6 fusion.2
  648.3 0.0 all-gather.4.cloned.1.call-update
  648.3 175.9 %all-gather.8.cloned.1.call-done = bf16[2,4096,1280]{2,1,0:T(8,128)(2,1)} async-done(((bf16[2,512,1280]{2,1,0:T(8,128)(2,1)}), bf16[2,4096,1280]{2,1,0:T(8,128)(2,1)}) %all-gather.8.cloned.1.call-update) | async-done | bytes 20971536 | tf_op jit(solution)/shard_map/all_gather | solution.py:21
  824.2 186.5 %all-gather.6.cloned.1.call-done = bf16[2,1280,4096]{2,1,0:T(8,128)(2,1)} async-done(((bf16[2,160,4096]{2,1,0:T(8,128)(2,1)}), bf16[2,1280,4096]{2,1,0:T(8,128)(2,1)}) %all-gather.6.cloned.1.call-update) | async-done | bytes 20971536 | tf_op jit(solution)/shard_map/all_gather | solution.py:21
  1010.7 186.5 %all-gather.4.cloned.1.call-done = bf16[2,1280,4096]{2,1,0:T(8,128)(2,1)} async-done(((bf16[2,160,4096]{2,1,0:T(8,128)(2,1)}), bf16[2,1280,4096]{2,1,0:T(8,128)(2,1)}) %all-gather.4.cloned.1.call-update) | async-done | bytes 20971536 | tf_op jit(solution)/shard_map/all_gather | solution.py:21
  1197.2 0.0 copy-start
  1197.2 0.0 slice-start
  1197.2 0.0 slice-start.1
  1197.2 0.0 slice-start.2
  1197.2 21.1 %copy.24 = bf16[2,1280,4096]{2,1,0:T(8,128)(2,1)} copy(bf16[2,1280,4096]{2,1,0:T(8,128)(2,1)} %all-gather.4.cloned.1.call-done) | data formatting | bytes 41943040
  1218.3 0.0 copy-done
  1218.3 0.0 slice-start.3
  1218.3 0.0 slice-start.4
  1218.3 10.6 copy.25
  1229.0 0.0 slice-done
  1229.0 0.0 slice-done.1
  1229.0 0.0 slice-done.2
  1229.0 1.6 slice-done.3
  1230.6 1.2 slice-done.4
  1231.8 7.5 copy.26
  (1 shorter events, 0.0 us)
Async XLA Ops:
  7.2 213.4 %reduce-scatter.8.cloned.1.call-start = ((), (), s32[]{:S(2)}) async-start(), calls=%async_computation.7 | async-start | bytes 23592960 | tf_op jit(solution)/shard_map/reduce_scatter | solution.py:17
  7.9 421.2 %reduce-scatter.6.cloned.1.call-start = ((), (), s32[]{:S(2)}) async-start(), calls=%async_computation.5 | async-start | bytes 23592960 | tf_op jit(solution)/shard_map/reduce_scatter | solution.py:17
  8.7 629.1 %reduce-scatter.4.cloned.1.call-start = ((), (), s32[]{:S(2)}) async-start(), calls=%async_computation.3 | async-start | bytes 23592960 | tf_op jit(solution)/shard_map/reduce_scatter | solution.py:17
  9.4 814.8 %all-gather.8.cloned.1.call-start = ((), (), s32[]{:S(2)}) async-start(), calls=%async_computation.8 | async-start | bytes 23592960 | tf_op jit(solution)/shard_map/all_gather | solution.py:21
  231.4 779.4 %all-gather.6.cloned.1.call-start = ((), (), s32[]{:S(2)}) async-start(), calls=%async_computation.6 | async-start | bytes 23592960 | tf_op jit(solution)/shard_map/all_gather | solution.py:21
  439.8 757.5 %all-gather.4.cloned.1.call-start = ((), (), s32[]{:S(2)}) async-start(), calls=%async_computation.4 | async-start | bytes 23592960 | tf_op jit(solution)/shard_map/all_gather | solution.py:21
  1197.2 21.1 %copy-start = (bf16[2,1280,4096]{2,1,0:T(8,128)(2,1)S(1)}, bf16[2,1280,4096]{2,1,0:T(8,128)(2,1)}, u32[]{:S(2)}) copy-start(bf16[2,1280,4096]{2,1,0:T(8,128)(2,1)} %all-gather.6.cloned.1.call-done) | copy-start | bytes 62914564
  1197.2 31.7 %slice-start = ((s8[20971520]{0:T(1024)(128)(4,1)}), s8[4194304]{0:T(1024)(128)(4,1)S(1)}, s32[]{:S(2)}) async-start(s8[20971520]{0:T(1024)(128)(4,1)} %bitcast.6), calls=%async_computation.9 | async-start | bytes 8388608
  1197.2 31.7 %slice-start.1 = ((s8[20971520]{0:T(1024)(128)(4,1)}), s8[4194304]{0:T(1024)(128)(4,1)S(1)}, s32[]{:S(2)}) async-start(s8[20971520]{0:T(1024)(128)(4,1)} %bitcast.6), calls=%async_computation.10 | async-start | bytes 8388608
  1197.2 31.7 %slice-start.2 = ((s8[20971520]{0:T(1024)(128)(4,1)}), s8[4194304]{0:T(1024)(128)(4,1)S(1)}, s32[]{:S(2)}) async-start(s8[20971520]{0:T(1024)(128)(4,1)} %bitcast.6), calls=%async_computation.11 | async-start | bytes 8388608
  1218.3 12.3 slice-start.3
  1218.3 13.4 %slice-start.4 = ((s8[20971520]{0:T(1024)(128)(4,1)}), s8[4194304]{0:T(1024)(128)(4,1)S(1)}, s32[]{:S(2)}) async-start(s8[20971520]{0:T(1024)(128)(4,1)} %bitcast.6), calls=%async_computation.13 | async-start | bytes 8388608
Sparse Core Ops, SparseCore 0:
  10.3 210.1 reduce-scatter.7
  222.9 206.1 reduce-scatter.5
  431.5 206.1 reduce-scatter.3
  639.8 184.4 all-gather.7
  826.3 184.4 all-gather.5
  1012.8 184.4 all-gather.3
where the time goes:
time: 1250 us
  waiting for transfers between devices  1160 us (93%)
  local copies, waits for them, and re-layouts  42.1 us (3%)
  other arithmetic  32 us (3%)
  between operations  14.1 us (1%)
    reduce_scatter x3, waiting for transfers between devices, step(): lax.psum_scatter(t[0], 'dp', scatter_dimension=1, tiled=True)  607 us
    all_gather x3, waiting for transfers between devices, step(): whole = [lax.all_gather(one[0], 'dp', axis=1, tiled=True) for one in new]  549 us
    unnamed x15, local copies, waits for them, and re-layouts  42.1 us
    convert_element_type x3, other arithmetic, adamw(): return ((w - 0.02 * step).astype(jnp.bfloat16), m, v)  32 us
  transfers between devices with their start and end apart: 6, of which 6 were waited for; matrix products, arithmetic and copies ran while one was open for 3% of the time, Pallas kernels for 0%

commit v1 on v0

v1 whole, which is shorter than its diff:
```python
import functools

import jax
import jax.numpy as jnp
from jax import lax
from jax.experimental import pallas as pl
from jax.experimental.pallas import tpu as pltpu
from jax.sharding import PartitionSpec as P

F32, BF16 = jnp.float32, jnp.bfloat16
MESH = pl.DeviceIdType.MESH
HOP = 3
SHIFT = (HOP - 1) // 2
AHEAD = 4
RING, FAR = 8, 16
ROWS = (16, 64)


def adamw(w, m, v, g):
    m = 0.9 * m + 0.1 * g
    v = 0.95 * v + 0.05 * g * g
    step = m * lax.rsqrt(v + 1e-8) + 0.1 * w
    return (w - 0.02 * step).astype(BF16), m, v


def kernel(*refs):
    grads, weights, m_in, v_in, w_out, m_out, v_out = (refs[i : i + 3] for i in range(0, 21, 3))
    own, par, rcv, snd, fin, wl, ml, vl = (refs[i : i + 2] for i in range(21, 37, 2))
    own_s, par_ss, par_rs, load_s, store_s, rs, ss, both_ss, both_rs = refs[37:]

    layers = m_in[0].shape[0]
    block = [m.shape[1] for m in m_in]
    per = [block[0] // ROWS[0], block[2] // ROWS[1]]
    first_down = 2 * layers * per[0]
    K = first_down + layers * per[1]

    dp = lax.axis_index("dp")
    z, core = dp // 2, dp % 2
    side = z // 2
    edge = (z == 0) | (z == 3)
    middle = jnp.logical_not(edge)
    inner = {"dp": 2 * (z + 1 - 2 * side) + core}
    outer_z = jnp.clip(z - 1 + 2 * side, 0, 3)
    outer = {"dp": 2 * outer_z + core}
    partner = {"dp": 2 * z + 1 - core}

    def owner(b):
        return 2 * (b + side * (3 - 2 * b)) + core

    def other(b):
        return 2 * (b + side * (3 - 2 * b)) + 1 - core

    def by_weight(c, do):
        n = layers * per[0]
        pl.when(c < n)(lambda: do(0, c // per[0], c % per[0]))
        pl.when((c >= n) & (c < 2 * n))(lambda: do(1, (c - n) // per[0], c % per[0]))
        pl.when(c >= 2 * n)(lambda: do(2, (c - 2 * n) // per[1], (c - 2 * n) % per[1]))

    def by_kind(c, do):
        pl.when(c < first_down)(lambda: do(0))
        pl.when(c >= first_down)(lambda: do(1))

    def rows_of(i, device, sub):
        h = ROWS[i // 2]
        return pl.ds(pl.multiple_of(device * block[i] + sub * h, h), h)

    def decode(pos):
        valid = (pos >= 0) & (pos < 4 * K)
        j = pos - (K - SHIFT)
        jc = jnp.maximum(j, 0)
        k, odd = jc // 2, jc % 2 == 1
        head, tail = valid & (j < 0), valid & (pos >= 3 * K + SHIFT)
        mid = valid & (j >= 0) & (pos < 3 * K + SHIFT)
        even = jnp.logical_not(odd)
        is_a = head | (mid & odd & (k < SHIFT))
        is_x = mid & even & (k < K)
        is_y = mid & odd & (k >= SHIFT)
        is_b = tail | (mid & even & (k >= K))
        in_mid = jnp.where(odd, jnp.where(k < SHIFT, K - SHIFT + k, k - SHIFT), jnp.where(k < K, k, k - K))
        return is_a, is_x, is_y, is_b, jnp.where(head, pos, jnp.where(tail, pos - 3 * K, in_mid))

    def pos_f(s):
        return s - jnp.where(edge, 0, HOP)

    def pos_g(s):
        return s - jnp.where(edge, 3 * HOP, 2 * HOP)

    def copy(src, dst, sem):
        return pltpu.make_async_copy(src, dst, sem)

    def remote(src, dst, send, recv, device):
        return pltpu.make_async_remote_copy(src_ref=src, dst_ref=dst, send_sem=send, recv_sem=recv, device_id=device, device_id_type=MESH)


    def tasks(s):
        fa, fx, fy, _, fc = decode(pos_f(s))
        ga, gx, _, _, gc = decode(pos_g(s))
        f_block = jnp.where(fa, 3, jnp.where(fx, 2, 1))
        g_block = jnp.where(ga, 0, 1)
        return ((0, fa | fx | (fy & edge), f_block, fc), (1, ga | (gx & middle), g_block, gc))

    def finals(s):
        ga, gx, _, _, gc = decode(pos_g(s))
        return (ga & edge) | (gx & middle), jnp.where(ga, 0, 1), gc

    def start_loads(s):
        near, far = s % RING, s % FAR
        for stream, wanted, b, c in tasks(s):

            @pl.when(wanted)
            def _(stream=stream, b=b, c=c):
                def go(i, layer, sub):
                    q = i // 2
                    copy(grads[i].at[layer, rows_of(i, owner(b), sub)], own[q].at[stream, near], own_s.at[stream, near]).start()
                    remote(
                        grads[i].at[layer, rows_of(i, other(b), sub)], par[q].at[stream, far],
                        par_ss.at[stream, near], par_rs.at[stream, far], partner,
                    ).start()

                by_weight(c, go)

        done, _, c = finals(s)

        @pl.when(done)
        def _():
            def go(i, layer, sub):
                q, h = i // 2, ROWS[i // 2]
                mine = pl.ds(pl.multiple_of(sub * h, h), h)
                copy(weights[i].at[layer, rows_of(i, dp, sub)], wl[q].at[near], load_s.at[0, near]).start()
                copy(m_in[i].at[layer, mine], ml[q].at[near], load_s.at[1, near]).start()
                copy(v_in[i].at[layer, mine], vl[q].at[near], load_s.at[2, near]).start()

            by_weight(c, go)

    def wait_loads(s, stream, c):
        near, far = s % RING, s % FAR

        def go(q):
            copy(own[q].at[stream, near], own[q].at[stream, near], own_s.at[stream, near]).wait()
            remote(par[q].at[stream, far], par[q].at[stream, far], par_ss.at[stream, near], par_rs.at[stream, far], partner).wait_recv()

        by_kind(c, go)

    def wait_given(s):
        near, far = s % RING, s % FAR
        for stream, wanted, _, c in tasks(s):

            @pl.when(wanted)
            def _(stream=stream, c=c):
                by_kind(c, lambda q: remote(par[q].at[stream, far], par[q].at[stream, far], par_ss.at[stream, near], par_rs.at[stream, far], partner).wait_send())


    def main_sends(s):
        near = s % RING
        pf, pg = pos_f(s), pos_g(s)
        fa, fx, fy, fb, fc = decode(pf)
        ga, gx, gy, gb, gc = decode(pg)
        f_ring = jnp.where(edge, 0, 1)

        def sums(stream):
            return lambda i: snd[i // 2].at[stream, near]

        return (
            ("sum", fa | fx | (fy & edge), fc, 0, inner, f_ring, pf % FAR, None),
            ("new", fy & middle, fc, 0, inner, f_ring, pf % FAR, 1),
            ("old", fb, fc, 0, inner, f_ring, pf % FAR, 0),
            ("sum", ga & middle, gc, 1, outer, 1, pg % FAR, None),
            ("new", gx & middle, gc, 1, outer, 1, pg % FAR, 1),
            ("old", (gy | gb) & middle, gc, 1, outer, 1, pg % FAR, jnp.where(gy, 2, 3)),
        )

    def start_send(s, entry):
        near = s % RING
        what, when, c, stream, device, ring, far, b = entry

        @pl.when(when)
        def _():
            if what == "sum":

                def go(q):
                    remote(snd[q].at[stream, near], rcv[q].at[ring, far], ss.at[stream, near], rs.at[ring, far], device).start()

                by_kind(c, go)
            else:

                def go(i, layer, sub):
                    place = w_out[i].at[layer, rows_of(i, owner(b), sub)]
                    src = fin[i // 2].at[near] if what == "new" else place
                    remote(src, place, ss.at[stream, near], rs.at[ring, far], device).start()

                by_weight(c, go)

    def shares(s):
        fa, fx, fy, fb, fc = decode(pos_f(s))
        ga, gx, gy, gb, gc = decode(pos_g(s))
        done, b, c = finals(s)
        return (
            (done, c, 0, "new", b),
            (fb & middle, fc, 1, "old", 0),
            (gy | gb | (gx & edge), gc, 2, "old", jnp.where(gy, 2, jnp.where(gb, 3, 1))),
        )

    def start_share(s, entry):
        near, far = s % RING, s % FAR
        when, c, which, what, b = entry

        @pl.when(when)
        def _():
            def go(i, layer, sub):
                place = w_out[i].at[layer, rows_of(i, owner(b), sub)]
                src = fin[i // 2].at[near] if what == "new" else place
                remote(src, place, both_ss.at[which, near], both_rs.at[which, far], partner).start()

            by_weight(c, go)

    def some(q):
        return fin[q].at[0]

    def wait_sends(s):
        near, far = s % RING, s % FAR
        for stream, entries in ((0, main_sends(s)[:3]), (1, main_sends(s)[3:])):
            when = functools.reduce(lambda a, b: a | b, [e[1] for e in entries])

            @pl.when(when)
            def _(stream=stream, c=entries[0][2]):
                by_kind(c, lambda q: remote(some(q), some(q), ss.at[stream, near], rs.at[0, 0], inner).wait_send())

        for when, c, which, _, _ in shares(s):

            @pl.when(when)
            def _(c=c, which=which):
                by_kind(c, lambda q: remote(some(q), some(q), both_ss.at[which, near], both_rs.at[which, far], partner).wait_send())

    def wait_shares(s):
        near, far = s % RING, s % FAR
        for when, c, which, _, _ in shares(s):

            @pl.when(when)
            def _(c=c, which=which):
                by_kind(c, lambda q: remote(some(q), some(q), both_ss.at[which, near], both_rs.at[which, far], partner).wait_recv())

    def wait_main(ring, pos, when, c):
        far = pos % FAR

        @pl.when(when)
        def _():
            by_kind(c, lambda q: remote(rcv[q].at[ring, far], rcv[q].at[ring, far], ss.at[0, 0], rs.at[ring, far], inner).wait_recv())

    def tiles(q, do):
        h, n = rcv[q].shape[2:]
        if q == 0:
            width = min(n, 512)

            @pl.loop(0, n // width)
            def _(i):
                do((slice(None), pl.ds(pl.multiple_of(i * width, width), width)))
        else:

            @pl.loop(0, h // 16)
            def _(i):
                do((pl.ds(pl.multiple_of(i * 16, 16), 16), slice(None)))

    def add(s, stream, pos, c, received):
        near, far = s % RING, s % FAR

        def go(q):
            def tile(at):
                total = own[q][(stream, near, *at)].astype(F32) + par[q][(stream, far, *at)].astype(F32)
                if received:
                    total = total + rcv[q][(stream, pos % FAR, *at)].astype(F32)
                snd[q][(stream, near, *at)] = total.astype(BF16)

            tiles(q, tile)

        by_kind(c, go)

    def finish(s, c, both):
        near, far = s % RING, s % FAR
        pf, pg = pos_f(s), pos_g(s)

        def loaded(q):
            for n, buf in enumerate((wl, ml, vl)):
                copy(buf[q].at[near], buf[q].at[near], load_s.at[n, near]).wait()

            def tile(at):
                total = own[q][(1, near, *at)].astype(F32) + par[q][(1, far, *at)].astype(F32)
                total = total + rcv[q][(1, pg % FAR, *at)].astype(F32)
                if both:
                    total = total + rcv[q][(0, pf % FAR, *at)].astype(F32)
                g = total.astype(BF16).astype(F32)
                w, m, v = adamw(wl[q][(near, *at)].astype(F32), ml[q][(near, *at)], vl[q][(near, *at)], g)
                fin[q][(near, *at)] = w
                ml[q][(near, *at)] = m
                vl[q][(near, *at)] = v

            tiles(q, tile)

        by_kind(c, loaded)

    def store(s, c):
        near = s % RING

        def go(i, layer, sub):
            q, h = i // 2, ROWS[i // 2]
            mine = pl.ds(pl.multiple_of(sub * h, h), h)
            copy(fin[q].at[near], w_out[i].at[layer, rows_of(i, dp, sub)], store_s.at[0, near]).start()
            copy(ml[q].at[near], m_out[i].at[layer, mine], store_s.at[1, near]).start()
            copy(vl[q].at[near], v_out[i].at[layer, mine], store_s.at[2, near]).start()

        by_weight(c, go)

    def wait_stores(s):
        near = s % RING
        done, _, c = finals(s)

        @pl.when(done)
        def _():
            def go(q):
                for n, buf in enumerate((fin, ml, vl)):
                    copy(buf[q].at[near], buf[q].at[near], store_s.at[n, near]).wait()

            by_kind(c, go)

    barrier = pltpu.get_barrier_semaphore()
    for device in (inner, partner):
        pl.semaphore_signal(barrier, inc=1, device_id=device, device_id_type=MESH)

    @pl.when(middle)
    def _():
        pl.semaphore_signal(barrier, inc=1, device_id=outer, device_id_type=MESH)
        pl.semaphore_wait(barrier, 3)

    @pl.when(edge)
    def _():
        pl.semaphore_wait(barrier, 2)

    @pl.loop(0, AHEAD)
    def _(s):
        start_loads(s)

    @pl.loop(0, 4 * K + 3 * HOP + 6)
    def _(s):
        pf, pg = pos_f(s), pos_g(s)
        fa, fx, fy, fb, fc = decode(pf)
        ga, gx, gy, gb, gc = decode(pg)
        sends, share = main_sends(s), shares(s)
        wait_stores(s - 2)
        wait_sends(s - 6)
        wait_given(s - 2)
        start_loads(s + AHEAD)
        wait_main(0, pf, (fa | fx | fy | fb) & middle, fc)
        start_send(s, sends[2])
        start_share(s, share[1])
        f_adds = fa | fx | (fy & edge)

        @pl.when(f_adds)
        def _():
            wait_loads(s, 0, fc)
            pl.when(edge)(lambda: add(s, 0, pf, fc, False))
            pl.when(middle)(lambda: add(s, 0, pf, fc, True))

        wait_main(1, pg, ga | gx | gy | gb, gc)
        start_send(s, sends[5])
        start_share(s, share[2])
        start_send(s, sends[0])
        last = (ga & edge) | (gx & middle)

        @pl.when(ga | (gx & middle))
        def _():
            wait_loads(s, 1, gc)

            @pl.when(ga & middle)
            def _():
                add(s, 1, pg, gc, True)

            pl.when(ga & edge)(lambda: finish(s, gc, False))
            pl.when(gx & middle)(lambda: finish(s, gc, True))

        wait_shares(s - 3)
        start_send(s, sends[1])
        start_send(s, sends[3])
        start_send(s, sends[4])
        start_share(s, share[0])
        pl.when(last)(lambda: store(s, gc))


def solution(mesh):
    def step(*arrays):
        terms, weights, m, v = (arrays[i : i + 3] for i in (0, 3, 6, 9))
        shapes = [(ROWS[q], weights[2 * q].shape[2]) for q in (0, 1)]

        def ring(*lead, dtype=BF16):
            return [pltpu.VMEM((*lead, *shape), dtype) for shape in shapes]

        def sems(*shape):
            return pltpu.SemaphoreType.DMA(shape)

        like = lambda x: jax.ShapeDtypeStruct(x.shape, x.dtype)
        anywhere = pl.BlockSpec(memory_space=pl.ANY)
        return pl.pallas_call(
            kernel,
            out_shape=[like(x) for x in (*weights, *m, *v)],
            in_specs=[anywhere] * 12,
            out_specs=[anywhere] * 9,
            scratch_shapes=[
                *ring(2, RING), *ring(2, FAR), *ring(2, FAR), *ring(2, RING), *ring(RING), *ring(RING),
                *ring(RING, dtype=F32), *ring(RING, dtype=F32),
                sems(2, RING), sems(2, RING), sems(2, FAR), sems(3, RING), sems(3, RING), sems(2, FAR), sems(2, RING), sems(3, RING), sems(3, FAR),
            ],
            compiler_params=pltpu.CompilerParams(collective_id=0, has_side_effects=True, vmem_limit_bytes=60 * 2**20),
        )(*(t[0] for t in terms), *weights, *m, *v)

    all_of, cut = P(None, None, None), P(None, "dp", None)
    return jax.shard_map(
        step,
        mesh=mesh,
        in_specs=(P(("rep", "dp"), None, None, None),) * 3 + (all_of,) * 3 + (cut,) * 6,
        out_specs=(P("rep", None, None),) * 3 + (P("rep", "dp", None),) * 6,
        check_vma=False,
    )
```

time: 1250 us -> 766 us (0.61)
  waiting for transfers between devices: 1160 us -> 0 us
  Pallas kernels: 0 us -> 700 us
  other arithmetic: 32 us -> 0.01 us
  local copies, waits for them, and re-layouts: 42.1 us -> 65.5 us
  between operations: 14.1 us -> 0.73 us
    pallas_call x0 -> x1, Pallas kernels: none -> 700 us  [step(): pl.pallas_call(kernel, out_shape=[like(x) for x in (*weights, *m, *v)], i...]
    reduce_scatter x3 -> x0, waiting for transfers between devices: 607 us -> none  [step(): lax.psum_scatter(t[0], 'dp', scatter_dimension=1, tiled=True)]
    all_gather x3 -> x0, waiting for transfers between devices: 549 us -> none  [step(): whole = [lax.all_gather(one[0], 'dp', axis=1, tiled=True) for one in new]]
    convert_element_type x3 -> x0, other arithmetic: 32 us -> none  [adamw(): return ((w - 0.02 * step).astype(jnp.bfloat16), m, v)]
    unnamed x15 -> x37, local copies, waits for them, and re-layouts: 42.1 us -> 65.5 us
  transfers between devices with their start and end apart: 6 -> 0, of which waited for: 6 -> 0; matrix products, arithmetic and copies ran while one was open for 3% -> 0% of each run, Pallas kernels for 0% -> 0%
where the time goes in v1:
time: 766 us
  Pallas kernels  700 us (91%)
  local copies, waits for them, and re-layouts  65.5 us (9%)
    pallas_call x1, Pallas kernels, step(): pl.pallas_call(kernel, out_shape=[like(x) for x in (*weights, *m, *v)], i...  700 us
    unnamed x37, local copies, waits for them, and re-layouts  65.5 us

profile of v1, /device:TPU:0, one launch (start us, length us, event | category | flops | bytes accessed | tf_op | source)
XLA Modules:
  0.0 766.2 jit_solution(14471931833585441670)
XLA Ops:
  0.6 700.0 %shard_map.187 = (bf16[2,1280,4096]{2,1,0:T(8,128)(2,1)}, bf16[2,1280,4096]{2,1,0:T(8,128)(2,1)}, bf16[2,4096,1280]{2,1,0:T(8,128)(2,1)}, f32[2,160,4096]{2,1,0:...) custom-call(bf16[2,1280,4096]{2,1,0:T(8,128)(2,1)} %bitcast.3, ...), custom_call_target="tpu_custom_call" | custom-call | tf_op jit(solution)/shard_map/pallas_call | solution.py:400
  700.6 0.0 copy-start
  700.7 0.0 slice-start
  700.7 0.0 slice-start.1
  700.7 0.0 slice-start.2
  700.7 21.1 %copy.30 = bf16[2,1280,4096]{2,1,0:T(8,128)(2,1)} copy(bf16[2,1280,4096]{2,1,0:T(8,128)(2,1)} %get-tuple-element.18) | data formatting | bytes 41943040
  721.8 0.0 copy-done
  721.8 0.0 slice-start.3
  721.8 0.0 slice-start.4
  721.8 0.0 slice-start.11
  721.8 10.6 %copy.31 = bf16[2,1280,4096]{2,1,0:T(8,128)(2,1)} copy(bf16[2,1280,4096]{2,1,0:T(8,128)(2,1)S(1)} %copy-done) | data formatting | bytes 41943040
  732.4 0.0 slice-done
  732.4 0.0 slice-done.1
  732.4 0.0 slice-done.2
  732.4 1.5 slice-done.3
  734.0 1.2 slice-done.4
  735.2 0.0 slice-start.12
  735.2 8.4 %copy.32 = bf16[2,4096,1280]{2,1,0:T(8,128)(2,1)} copy(bf16[2,4096,1280]{2,1,0:T(8,128)(2,1)S(1)} %bitcast.7) | data formatting | bytes 41943040
  743.6 5.4 copy.33
  749.1 0.0 slice-start.9
  749.1 0.0 slice-start.7
  749.1 5.9 copy.34
  755.0 0.0 slice-done.11
  755.0 0.0 slice-done.12
  755.0 0.0 slice-start.10
  755.0 0.0 slice-start.8
  755.0 2.5 copy.35
  757.4 0.0 slice-done.9
  757.4 0.0 slice-done.10
  757.4 0.0 slice-start.5
  757.4 2.7 copy.36
  760.1 0.0 slice-done.7
  760.1 0.0 slice-done.8
  760.1 0.0 slice-start.6
  760.1 2.7 copy.37
  762.8 0.0 slice-done.5
  762.8 1.0 slice-done.6
  763.8 2.4 copy.38
  (5 shorter events, 0.0 us)
Async XLA Ops:
  700.6 21.2 %copy-start = (bf16[2,1280,4096]{2,1,0:T(8,128)(2,1)S(1)}, bf16[2,1280,4096]{2,1,0:T(8,128)(2,1)}, u32[]{:S(2)}) copy-start(bf16[2,1280,4096]{2,1,0:T(8,128)(2,1)} %get-tuple-element.19) | copy-start | bytes 62914564
  700.7 31.8 %slice-start = ((s8[20971520]{0:T(1024)(128)(4,1)}), s8[4194304]{0:T(1024)(128)(4,1)S(1)}, s32[]{:S(2)}) async-start(s8[20971520]{0:T(1024)(128)(4,1)} %bitcast.6), calls=%async_computation | async-start | bytes 8388608
  700.7 31.8 %slice-start.1 = ((s8[20971520]{0:T(1024)(128)(4,1)}), s8[4194304]{0:T(1024)(128)(4,1)S(1)}, s32[]{:S(2)}) async-start(s8[20971520]{0:T(1024)(128)(4,1)} %bitcast.6), calls=%async_computation.1 | async-start | bytes 8388608
  700.7 31.8 %slice-start.2 = ((s8[20971520]{0:T(1024)(128)(4,1)}), s8[4194304]{0:T(1024)(128)(4,1)S(1)}, s32[]{:S(2)}) async-start(s8[20971520]{0:T(1024)(128)(4,1)} %bitcast.6), calls=%async_computation.2 | async-start | bytes 8388608
  721.8 12.2 %slice-start.3 = ((s8[20971520]{0:T(1024)(128)(4,1)}), s8[4194304]{0:T(1024)(128)(4,1)S(1)}, s32[]{:S(2)}) async-start(s8[20971520]{0:T(1024)(128)(4,1)} %bitcast.6), calls=%async_computation.3 | async-start | bytes 8388608
  721.8 13.4 %slice-start.4 = ((s8[20971520]{0:T(1024)(128)(4,1)}), s8[4194304]{0:T(1024)(128)(4,1)S(1)}, s32[]{:S(2)}) async-start(s8[20971520]{0:T(1024)(128)(4,1)} %bitcast.6), calls=%async_computation.4 | async-start | bytes 8388608
  721.8 33.2 %slice-start.11 = ((s8[5242880]{0:T(1024)(128)(4,1)}), s8[1048576]{0:T(1024)(128)(4,1)S(1)}, s32[]{:S(2)}) async-start(s8[5242880]{0:T(1024)(128)(4,1)} %bitcast.14), calls=%async_computation.11 | async-start | bytes 2097152
  735.2 19.8 %slice-start.12 = ((s8[5242880]{0:T(1024)(128)(4,1)}), s8[4194304]{0:T(1024)(128)(4,1)S(1)}, s32[]{:S(2)}) async-start(s8[5242880]{0:T(1024)(128)(4,1)} %bitcast.14), calls=%async_computation.12 | async-start | bytes 8388608
  749.1 8.4 %slice-start.9 = ((s8[5242880]{0:T(1024)(128)(4,1)}), s8[4194304]{0:T(1024)(128)(4,1)S(1)}, s32[]{:S(2)}) async-start(s8[5242880]{0:T(1024)(128)(4,1)} %bitcast.12), calls=%async_computation.9 | async-start | bytes 8388608
  749.1 11.1 %slice-start.7 = ((s8[5242880]{0:T(1024)(128)(4,1)}), s8[4194304]{0:T(1024)(128)(4,1)S(1)}, s32[]{:S(2)}) async-start(s8[5242880]{0:T(1024)(128)(4,1)} %bitcast.10), calls=%async_computation.7 | async-start | bytes 8388608
  755.0 2.5 slice-start.10
  755.0 5.1 slice-start.8
  757.4 5.3 slice-start.5
  760.1 3.7 slice-start.6
